TPU v7x, 256 devices: a whole 4x4x8 slice. The times are simulated.
256 devices in a mesh: row: 8 (over y, core), col: 32 (over z, x).
Axes of the slice: x: 4, y: 4, z: 8, core: 2. Of those that a mesh axis runs over, the one named last changes fastest.
Arguments:
- factor: float32 [6, 2048, 6, 2048], P(None, 'row', None, 'col'), may hold values from -0.0625 to 0.0625
- diag_inv: float32 [6, 2048, 2048], P(None, None, 'row'), may hold values from -2 to 2, as said below
- structure: int32 [6, 6, 16], P(None, None, 'row'), may hold values 0 or 1
- parent: int32 [6], replicated, may hold values from 1 to 6, as said below
- post: float32 [6, 2048, 64], P(None, 'row', 'col'), may hold values from -6 to 6
Outputs:
- mean_x: float32 [6, 2048, 64], P(None, 'row', 'col')
- variance: float32 [6, 2048], P(None, 'row')
Inputs may be any that keep to these rules, and one draw needn't show every extreme that they name: parent[s] > s for s < 5, and parent[5] = 6; every supernode has at most 2 ancestors, and some supernode has exactly that many. The diagonal of each diag_inv[s] lies in 0.5 to 2.
All inputs are finite; a program needn't handle non-finite values. No bound on the sum of `structure` on one device may be relied on, other than what follows from the above.
Results may differ from a plain program's by a relative error of at most 0.00014.
Values sent between devices are 32-bit elements; how exact they have to be, the bound alone decides.
No kernel may reach another device: no remote copies, remote signals or barrier semaphores. Data moves between devices by JAX's collectives and lax.ppermute only.
A program may use at most 128 MiB of HBM per device.

v0:
```python
import jax
import jax.numpy as jnp
from jax import lax
from jax.sharding import Mesh
from jax.sharding import PartitionSpec as P

LEVELS = 3
COL = ("col_0", "col_1")
HIGHEST = lax.Precision.HIGHEST


def laid_out(parts, dim):
    parts = jnp.moveaxis(parts, 0, dim)
    dims = parts.shape
    return parts.reshape(*dims[:dim], dims[dim] * dims[dim + 1], *dims[dim + 2 :])


def from_everyone(array, axis):
    copies = jnp.broadcast_to(array, (lax.axis_size(axis), *array.shape))
    return lax.all_to_all(copies, axis, split_axis=0, concat_axis=0, tiled=True)


def gathered_copies(array, axis, dim):
    return laid_out(from_everyone(array, axis), dim)


def filled_up(lines, peers):
    spare = -len(lines) % peers
    return jnp.pad(lines, [(0, spare)] + [(0, 0)] * (lines.ndim - 1))


def total_of(array, axis):
    lines = array.reshape(-1, *array.shape[1:][-1:])
    padded = filled_up(lines, lax.axis_size(axis))
    own = lax.psum_scatter(padded, axis, scatter_dimension=0, tiled=True)
    whole = lax.all_gather(own, axis, axis=0, tiled=True)
    return whole[: len(lines)].reshape(array.shape)


def gathered_by_axis(array, axes, dim):
    if not axes:
        return array
    nearer = lax.all_gather(array, axes[-1], axis=dim, tiled=True)
    return gathered_by_axis(nearer, axes[:-1], dim)


def taken_together(array, axis):
    everything = from_everyone(array, axis)
    return jnp.sum(everything, axis=0)


def contract(selected, panel_piece):
    return jnp.einsum("tiw,tin->wn", panel_piece, selected, precision=HIGHEST)


def body(factor, diag_inv, structure, parent, post):
    super_count = factor.shape[0]
    row_width = factor.shape[1]
    col_width = factor.shape[3]
    full_width = diag_inv.shape[1]
    rhs_width = post.shape[2]
    row_at = lax.axis_index("row")
    col_at = lax.axis_index(COL)
    extended = jnp.concatenate([parent, jnp.full((1,), super_count, jnp.int32)])
    slot_ids = jnp.arange(super_count + 1, dtype=jnp.int32)
    targets = jnp.arange(super_count, dtype=jnp.int32)
    ancestor_hops = []
    current = parent
    for hop_index in range(super_count - 1):
        ancestor_hops.append(current)
        onehot = (current[:, None] == slot_ids[None, :]).astype(jnp.int32)
        current = jnp.sum(onehot * extended[None, :], axis=1)
    ancestry = jnp.zeros((super_count, super_count), jnp.float32)
    for hop_targets in ancestor_hops:
        ancestry = ancestry + (hop_targets[:, None] == targets[None, :]).astype(jnp.float32)
    block_rows = row_width // structure.shape[2]
    row_mask = jnp.repeat(structure.astype(jnp.float32), block_rows, axis=2) * ancestry[:, :, None]
    masked = factor * jnp.transpose(row_mask, (1, 2, 0))[:, :, :, None]
    rows_full = jnp.arange(full_width, dtype=jnp.int32)
    own_cols = row_at * row_width + jnp.arange(row_width, dtype=jnp.int32)
    lower_inv = jnp.where((rows_full[:, None] >= own_cols[None, :])[None, :, :], diag_inv, 0.0)
    unit_cols = col_at * col_width + jnp.arange(col_width, dtype=jnp.int32)
    unit_block = (rows_full[:, None] == unit_cols[None, :]).astype(jnp.float32)
    gathered = gathered_copies(post, "row", 1)
    total_cols = super_count * col_width + rhs_width
    solution = jnp.zeros((super_count, row_width, total_cols), jnp.float32)
    for current_sup in range(super_count - 1, -1, -1):
        later_cols = (current_sup + 1) * col_width
        if current_sup == super_count - 1:
            summed = jnp.zeros((full_width, rhs_width), jnp.float32)
        else:
            picks = []
            chosen_rows = []
            for slot_index in range(LEVELS - 1):
                target = ancestor_hops[slot_index][current_sup]
                is_valid = (target < super_count).astype(jnp.float32)
                clamped = jnp.minimum(target, super_count - 1)
                picks.append(
                    lax.dynamic_index_in_dim(
                        masked[:, :, current_sup, :], clamped, 0, keepdims=False
                    )
                    * is_valid
                )
                chosen_rows.append(
                    lax.dynamic_index_in_dim(solution, clamped, 0, keepdims=False)[:, later_cols:]
                )
            blocks = jnp.stack(picks)
            selected = jnp.stack(chosen_rows)
            partial_value = contract(selected, gathered_by_axis(blocks, COL, 2))
            summed = total_of(partial_value, "row")
        split_at = summed.shape[1] - rhs_width
        remaining = jnp.concatenate(
            [-summed[:, :split_at], gathered[current_sup] - summed[:, split_at:]], axis=1
        )
        right = jnp.concatenate([unit_block, remaining], axis=1)
        fresh = jnp.dot(
            lower_inv[current_sup].T, right, precision=HIGHEST, preferred_element_type=jnp.float32
        )
        solution = solution.at[current_sup, :, current_sup * col_width :].set(fresh)
    mean_x = solution[:, :, super_count * col_width :]
    unit_part = solution[:, :, : super_count * col_width]
    squares = jnp.sum(unit_part * unit_part, axis=2)
    variance = taken_together(squares, COL)
    return (mean_x, variance)


def solution(mesh):
    finer = Mesh(mesh.devices.reshape(mesh.shape["row"], 8, 4), ("row", "col_0", "col_1"))
    placed = (
        P(None, "row", None, COL),
        P(None, None, "row"),
        P(None, None, "row"),
        P(),
        P(None, "row", COL),
    )
    return jax.shard_map(
        body,
        mesh=finer,
        in_specs=placed,
        out_specs=(P(None, "row", COL), P(None, "row")),
        check_vma=False,
    )
```

profile of v0, /device:TPU:8, one launch (start us, length us, event | category | flops | bytes accessed | tf_op | source)
XLA Modules:
  0.0 674.4 jit_solution(18095809335935411941)
XLA Ops:
  20.2 13.1 %all_gather.45 = f32[2,256,256]{1,0,2:T(2,128)S(1)} all-gather(f32[2,256,64]{1,0,2:T(2,128)S(1)} %pad_maximum_fusion), channel_id=1, replica_groups=mesh['row'=8,'col_0'=8,'col_1'=4] {'col_1'}, dimensions={2}, use_global_device_ids=true | all-gather | bytes 655360 | tf_op jit(solution)/shard_map/all_gather | solution.py:43
  41.1 10.7 %broadcast_select_fusion = f32[6,2048,256]{2,1,0:T(8,128)} fusion(f32[6,2048,256]{2,1,0:T(8,128)} %param.18, pred[2048,256]{1,0:T(8,128)(4,1)S(1)} %iota_compare_fusion), kind=kLoop, calls=%fused_computation | loop fusion | flops 3145728 | bytes 25690112 | tf_op jit(solution)/shard_map/jit(_where)/select_n | solution.py:81
  55.6 36.5 %all-gather.10.cloned.1.call-done = f32[2,256,2048]{2,1,0:T(8,128)} async-done(((f32[2,256,256]{2,1,0:T(8,128)}), f32[2,256,2048]{2,1,0:T(8,128)}) %all-gather.10.cloned.1.call-update) | async-done | bytes 4194320 | tf_op jit(solution)/shard_map/all_gather | solution.py:43
  103.3 13.1 %all_gather.48 = f32[2,256,256]{1,0,2:T(2,128)S(1)} all-gather(f32[2,256,64]{1,0,2:T(2,128)S(1)} %pad_maximum_fusion.1), channel_id=1, replica_groups=mesh['row'=8,'col_0'=8,'col_1'=4] {'col_1'}, dimensions={2}, use_global_device_ids=true | all-gather | bytes 655360 | tf_op jit(solution)/shard_map/all_gather | solution.py:43
  117.6 10.2 %reduce-scatter.6.cloned.1.call-done = f32[256,66]{0,1:T(8,128)} async-done(((f32[2048,66]{0,1:T(8,128)}), f32[256,66]{0,1:T(8,128)}) %reduce-scatter.6.cloned.1.call-update) | async-done | bytes 67600 | tf_op jit(solution)/shard_map/reduce_scatter | solution.py:35
  127.9 14.5 %all_gather.47 = f32[2048,66]{0,1:T(8,128)S(1)} all-gather(f32[256,66]{0,1:T(8,128)} %reduce-scatter.6.cloned.1.call-done), channel_id=1, replica_groups=mesh['row'=8,'col_0'=8,'col_1'=4] {'row'}, dimensions={0}, use_global_device_ids=true | all-gather | bytes 608256 | tf_op jit(solution)/shard_map/all_gather | solution.py:36
  145.5 40.6 %all-gather.12.cloned.1.call-done = f32[2,256,2048]{2,1,0:T(8,128)} async-done(((f32[2,256,256]{2,1,0:T(8,128)}), f32[2,256,2048]{2,1,0:T(8,128)}) %all-gather.12.cloned.1.call-update) | async-done | bytes 4194320 | tf_op jit(solution)/shard_map/all_gather | solution.py:43
  191.9 30.6 %reduce-scatter.8.cloned.1.call-done = f32[256,130]{0,1:T(8,128)} async-done(((f32[2048,130]{0,1:T(8,128)}), f32[256,130]{0,1:T(8,128)}) %reduce-scatter.8.cloned.1.call-update) | async-done | bytes 133136 | tf_op jit(solution)/shard_map/reduce_scatter | solution.py:35
  222.7 13.2 %all_gather.51 = f32[2,256,256]{1,0,2:T(2,128)S(1)} all-gather(f32[2,256,64]{1,0,2:T(2,128)S(1)} %pad_maximum_fusion.2), channel_id=1, replica_groups=mesh['row'=8,'col_0'=8,'col_1'=4] {'col_1'}, dimensions={2}, use_global_device_ids=true | all-gather | bytes 655360 | tf_op jit(solution)/shard_map/all_gather | solution.py:43
  237.0 13.5 %all-gather.14.cloned.1.call-done = f32[2048,130]{0,1:T(8,128)} async-done(((f32[256,130]{0,1:T(8,128)}), f32[2048,130]{0,1:T(8,128)}) %all-gather.14.cloned.1.call-update) | async-done | bytes 1064976 | tf_op jit(solution)/shard_map/all_gather | solution.py:36
  255.9 52.6 %all-gather.16.cloned.1.call-done = f32[2,256,2048]{2,1,0:T(8,128)} async-done(((f32[2,256,256]{2,1,0:T(8,128)}), f32[2,256,2048]{2,1,0:T(8,128)}) %all-gather.16.cloned.1.call-update) | async-done | bytes 4194320 | tf_op jit(solution)/shard_map/all_gather | solution.py:43
  315.2 31.2 %reduce-scatter.10.cloned.1.call-done = f32[256,194]{0,1:T(8,128)} async-done(((f32[2048,194]{0,1:T(8,128)}), f32[256,194]{0,1:T(8,128)}) %reduce-scatter.10.cloned.1.call-update) | async-done | bytes 198672 | tf_op jit(solution)/shard_map/reduce_scatter | solution.py:35
  354.1 13.2 %all_gather.54 = f32[2,256,256]{1,0,2:T(2,128)S(1)} all-gather(f32[2,256,64]{1,0,2:T(2,128)S(1)} %pad_maximum_fusion.3), channel_id=1, replica_groups=mesh['row'=8,'col_0'=8,'col_1'=4] {'col_1'}, dimensions={2}, use_global_device_ids=true | all-gather | bytes 655360 | tf_op jit(solution)/shard_map/all_gather | solution.py:43
  381.8 52.3 %all-gather.20.cloned.1.call-done = f32[2,256,2048]{2,1,0:T(8,128)} async-done(((f32[2,256,256]{2,1,0:T(8,128)}), f32[2,256,2048]{2,1,0:T(8,128)}) %all-gather.20.cloned.1.call-update) | async-done | bytes 4194320 | tf_op jit(solution)/shard_map/all_gather | solution.py:43
  434.1 7.5 %convolution_bitcast_fusion.1 = f32[2048,258]{0,1:T(8,128)} fusion(f32[2,256,2048]{2,1,0:T(8,128)} %all-gather.20.cloned.1.call-done, f32[1,256,258]{1,2,0:T(8,128)S(1)} %slice_bitcast_fusion.36, f32[1,256,258]{1,2,0:T(8,128)S(1)} %slice_bitcast_fusion.37), kind=kOutput, calls=%fused_computation.9 | convolution fusion | flops 3246523392 | bytes 6836224 | tf_op jit(solution)/shard_map/tiw,tin->wn/dot_general | solution.py:53
  441.7 32.1 %reduce-scatter.12.cloned.1.call-done = f32[256,258]{0,1:T(8,128)} async-done(((f32[2048,258]{0,1:T(8,128)}), f32[256,258]{0,1:T(8,128)}) %reduce-scatter.12.cloned.1.call-update) | async-done | bytes 264208 | tf_op jit(solution)/shard_map/reduce_scatter | solution.py:35
  474.0 13.1 %all_gather.57 = f32[2,256,256]{1,0,2:T(2,128)S(1)} all-gather(f32[2,256,64]{1,0,2:T(2,128)S(1)} %pad_maximum_fusion.4), channel_id=1, replica_groups=mesh['row'=8,'col_0'=8,'col_1'=4] {'col_1'}, dimensions={2}, use_global_device_ids=true | all-gather | bytes 655360 | tf_op jit(solution)/shard_map/all_gather | solution.py:43
  488.4 16.2 %all-gather.22.cloned.1.call-done = f32[2048,258]{0,1:T(8,128)} async-done(((f32[256,258]{0,1:T(8,128)}), f32[2048,258]{0,1:T(8,128)}) %all-gather.22.cloned.1.call-update) | async-done | bytes 2113552 | tf_op jit(solution)/shard_map/all_gather | solution.py:36
  512.0 50.5 %all-gather.24.cloned.1.call-done = f32[2,256,2048]{2,1,0:T(8,128)} async-done(((f32[2,256,256]{2,1,0:T(8,128)}), f32[2,256,2048]{2,1,0:T(8,128)}) %all-gather.24.cloned.1.call-update) | async-done | bytes 4194320 | tf_op jit(solution)/shard_map/all_gather | solution.py:43
  562.5 8.3 %convolution_bitcast_fusion = f32[2048,322]{0,1:T(8,128)} fusion(f32[2,256,2048]{2,1,0:T(8,128)} %all-gather.24.cloned.1.call-done, f32[1,256,322]{1,2,0:T(8,128)S(1)} %slice_bitcast_fusion.34, f32[1,256,322]{1,2,0:T(8,128)} %slice_bitcast_fusion.35), kind=kOutput, calls=%fused_computation.8 | convolution fusion | flops 4051862528 | bytes 7491584 | tf_op jit(solution)/shard_map/tiw,tin->wn/dot_general | solution.py:53
  570.9 33.1 %reduce-scatter.14.cloned.1.call-done = f32[256,322]{0,1:T(8,128)} async-done(((f32[2048,322]{0,1:T(8,128)}), f32[256,322]{0,1:T(8,128)}) %reduce-scatter.14.cloned.1.call-update) | async-done | bytes 329744 | tf_op jit(solution)/shard_map/reduce_scatter | solution.py:35
  604.0 31.8 %all-gather.26.cloned.1.call-done = f32[2048,322]{0,1:T(8,128)} async-done(((f32[256,322]{0,1:T(8,128)}), f32[2048,322]{0,1:T(8,128)}) %all-gather.26.cloned.1.call-update) | async-done | bytes 2637840 | tf_op jit(solution)/shard_map/all_gather | solution.py:36
  643.8 9.8 %all-to-all-start.1 = ((f32[32,6,256]{2,1,0:T(8,128)}), f32[32,6,256]{2,1,0:T(8,128)S(1)}, u32[]{:S(2)}, u32[]{:S(2)}) async-start(f32[32,6,256]{2,1,0:T(8,128)} %broadcast_in_dim.18), calls=%async_computation.6 | async-start | bytes 524288 | tf_op jit(solution)/shard_map/all_to_all | solution.py:20
  654.3 12.8 %all-to-all-done.1 = f32[32,6,256]{2,1,0:T(8,128)S(1)} async-done(((f32[32,6,256]{2,1,0:T(8,128)}), f32[32,6,256]{2,1,0:T(8,128)S(1)}, u32[]{:S(2)}, u32[]{:S(2)}) %all-to-all-start.1) | async-done | bytes 196640 | tf_op jit(solution)/shard_map/all_to_all | solution.py:20
  (109 shorter events, 87.1 us)
Async XLA Ops:
  7.2 84.9 %all-gather.10.cloned.1.call-start = ((), (), s32[]{:S(2)}) async-start(), calls=%async_computation.7 | async-start | bytes 4718592 | tf_op jit(solution)/shard_map/all_gather | solution.py:43
  19.9 14.4 %copy-start.2 = (f32[6,256,2]{1,2,0:T(2,128)S(1)}, f32[6,256,2]{1,2,0:T(2,128)}, u32[]{:S(2)}) copy-start(f32[6,256,2]{1,2,0:T(2,128)} %param.21) | copy-start | bytes 36868
  35.0 16.9 %all-to-all-start = ((f32[8,6,256,2]{2,3,1,0:T(2,128)}), f32[8,6,256,2]{2,3,1,0:T(2,128)S(1)}, u32[]{:S(2)}, u32[]{:S(2)}) async-start(f32[8,6,256,2]{2,3,1,0:T(2,128)} %broadcast_in_dim.16), calls=%async_computation | async-start | bytes 196608 | tf_op jit(solution)/shard_map/all_to_all | solution.py:20
  40.7 87.1 %reduce-scatter.6.cloned.1.call-start = ((), (), s32[]{:S(2)}) async-start(), calls=%async_computation.8 | async-start | bytes 663552 | tf_op jit(solution)/shard_map/reduce_scatter | solution.py:35
  97.9 88.3 %all-gather.12.cloned.1.call-start = ((), (), s32[]{:S(2)}) async-start(), calls=%async_computation.9 | async-start | bytes 4718592 | tf_op jit(solution)/shard_map/all_gather | solution.py:43
  117.4 105.1 %reduce-scatter.8.cloned.1.call-start = ((), (), s32[]{:S(2)}) async-start(), calls=%async_computation.10 | async-start | bytes 1253376 | tf_op jit(solution)/shard_map/reduce_scatter | solution.py:35
  191.9 58.6 %all-gather.14.cloned.1.call-start = ((), (), s32[]{:S(2)}) async-start(), calls=%async_computation.11 | async-start | bytes 1253376 | tf_op jit(solution)/shard_map/all_gather | solution.py:36
  222.5 86.1 %all-gather.16.cloned.1.call-start = ((), (), s32[]{:S(2)}) async-start(), calls=%async_computation.12 | async-start | bytes 4718592 | tf_op jit(solution)/shard_map/all_gather | solution.py:43
  236.9 109.5 %reduce-scatter.10.cloned.1.call-start = ((), (), s32[]{:S(2)}) async-start(), calls=%async_computation.13 | async-start | bytes 1843200 | tf_op jit(solution)/shard_map/reduce_scatter | solution.py:35
  315.2 60.5 %all-gather.18.cloned.1.call-start = ((), (), s32[]{:S(2)}) async-start(), calls=%async_computation.14 | async-start | bytes 1843200 | tf_op jit(solution)/shard_map/all_gather | solution.py:36
  346.5 87.6 %all-gather.20.cloned.1.call-start = ((), (), s32[]{:S(2)}) async-start(), calls=%async_computation.15 | async-start | bytes 4718592 | tf_op jit(solution)/shard_map/all_gather | solution.py:43
  368.5 105.3 %reduce-scatter.12.cloned.1.call-start = ((), (), s32[]{:S(2)}) async-start(), calls=%async_computation.16 | async-start | bytes 2433024 | tf_op jit(solution)/shard_map/reduce_scatter | solution.py:35
  441.6 32.2 %copy-start = (f32[1,256,64]{1,0,2:T(1,128)S(1)}, f32[1,256,64]{1,0,2:T(1,128)}, u32[]{:S(2)}) copy-start(f32[1,256,64]{1,0,2:T(1,128)} %get-tuple-element.88) | copy-start | bytes 196612
  441.6 63.0 %copy-start.1 = (f32[1,8,256,2]{2,3,0,1:T(2,128)S(1)}, f32[1,8,256,2]{2,3,0,1:T(2,128)}, u32[]{:S(2)}) copy-start(f32[1,8,256,2]{2,3,0,1:T(2,128)} %get-tuple-element.98) | copy-start | bytes 49156
  441.6 62.9 %all-gather.22.cloned.1.call-start = ((), (), s32[]{:S(2)}) async-start(), calls=%async_computation.17 | async-start | bytes 2433024 | tf_op jit(solution)/shard_map/all_gather | solution.py:36
  473.8 88.7 %all-gather.24.cloned.1.call-start = ((), (), s32[]{:S(2)}) async-start(), calls=%async_computation.18 | async-start | bytes 4718592 | tf_op jit(solution)/shard_map/all_gather | solution.py:43
  488.1 115.9 %reduce-scatter.14.cloned.1.call-start = ((), (), s32[]{:S(2)}) async-start(), calls=%async_computation.19 | async-start | bytes 3022848 | tf_op jit(solution)/shard_map/reduce_scatter | solution.py:35
  570.9 64.9 %all-gather.26.cloned.1.call-start = ((), (), s32[]{:S(2)}) async-start(), calls=%async_computation.20 | async-start | bytes 3022848 | tf_op jit(solution)/shard_map/all_gather | solution.py:36
  643.8 23.2 %all-to-all-start.1 = ((f32[32,6,256]{2,1,0:T(8,128)}), f32[32,6,256]{2,1,0:T(8,128)S(1)}, u32[]{:S(2)}, u32[]{:S(2)}) async-start(f32[32,6,256]{2,1,0:T(8,128)} %broadcast_in_dim.18), calls=%async_computation.6 | async-start | bytes 524288 | tf_op jit(solution)/shard_map/all_to_all | solution.py:20
Sparse Core Ops, SparseCore 0:
  34.5 57.5 all-gather.9
  98.0 29.8 reduce-scatter.5
  129.7 56.4 all-gather.11
  192.0 30.4 reduce-scatter.7
  224.2 26.2 all-gather.13
  252.1 56.4 all-gather.15
  315.3 31.1 reduce-scatter.9
  348.3 27.3 all-gather.17
  377.5 56.5 all-gather.19
  441.7 31.9 reduce-scatter.11
  475.6 28.8 all-gather.21
  506.2 56.2 all-gather.23
  571.0 32.9 reduce-scatter.13
  605.7 30.0 all-gather.25
where the time goes:
time: 683 us; the launch traced here: 674 us
  waiting for transfers between devices  451 us (66%)
  blocking collectives  80.2 us (12%)
  matrix products  54.9 us (8%)
  other arithmetic  32 us (5%)
  between operations  26.9 us (4%)
  starting transfers between devices  16.5 us (2%)
  local copies, waits for them, and re-layouts  12.8 us (2%)
    all_gather x5, waiting for transfers between devices, gathered_by_axis(): nearer = lax.all_gather(array, axes[-1], axis=dim, tiled=True)  233 us
    reduce_scatter x5, waiting for transfers between devices, total_of(): own = lax.psum_scatter(padded, axis, scatter_dimension=0, tiled=True)  137 us
    all_gather x4, waiting for transfers between devices, total_of(): whole = lax.all_gather(own, axis, axis=0, tiled=True)  68.4 us
    all_gather x5, blocking collectives, gathered_by_axis(): nearer = lax.all_gather(array, axes[-1], axis=dim, tiled=True)  65.7 us
    dot_general x5, matrix products, contract(): return jnp.einsum('tiw,tin->wn', panel_piece, selected, precision=HIGHEST)  33.9 us
    dot_general x6, matrix products, body(): jnp.dot(lower_inv[current_sup].T, right, precision=HIGHEST, preferred_ele...  21 us
    all_to_all x2, starting transfers between devices, from_everyone(): return lax.all_to_all(copies, axis, split_axis=0, concat_axis=0, tiled=True)  15.5 us
    all_gather x1, blocking collectives, total_of(): whole = lax.all_gather(own, axis, axis=0, tiled=True)  14.5 us
  transfers between devices with their start and end apart: 16, of which 15 were waited for; matrix products, arithmetic and copies ran while one was open for 7% of the time, Pallas kernels for 0%

commit v1 on v0

--- a/solution.py
+++ b/solution.py
@@ -33,7 +33,9 @@
     lines = array.reshape(-1, *array.shape[1:][-1:])
     padded = filled_up(lines, lax.axis_size(axis))
     own = lax.psum_scatter(padded, axis, scatter_dimension=0, tiled=True)
-    whole = lax.all_gather(own, axis, axis=0, tiled=True)
+    whole = jnp.concatenate(
+        lax.all_to_all(jnp.stack([own] * lax.axis_size(axis)), axis, 0, 0), axis=0
+    )
     return whole[: len(lines)].reshape(array.shape)
 
 

time: 683 us -> 603 us (0.88)
  waiting for transfers between devices: 451 us -> 252 us
  blocking collectives: 80.2 us -> 186 us
  local copies, waits for them, and re-layouts: 12.8 us -> 26.4 us
  other arithmetic: 32 us -> 24.4 us
    all_to_all x0 -> x4, blocking collectives: none -> 120 us  [total_of(): lax.all_to_all(jnp.stack([own] * lax.axis_size(axis)), axis, 0, 0)]
    all_gather x5, waiting for transfers between devices: 233 us -> 147 us  [gathered_by_axis(): nearer = lax.all_gather(array, axes[-1], axis=dim, tiled=True)]
    all_gather x4 -> x0, waiting for transfers between devices: 68.4 us -> none  [total_of(): whole = lax.all_gather(own, axis, axis=0, tiled=True)]
    reduce_scatter x5, waiting for transfers between devices: 137 us -> 85.1 us  [total_of(): own = lax.psum_scatter(padded, axis, scatter_dimension=0, tiled=True)]
    all_gather x1 -> x0, blocking collectives: 14.5 us -> none  [total_of(): whole = lax.all_gather(own, axis, axis=0, tiled=True)]
    all_to_all x0 -> x1, waiting for transfers between devices: none -> 8.35 us  [total_of(): lax.all_to_all(jnp.stack([own] * lax.axis_size(axis)), axis, 0, 0)]
    all_to_all x0 -> x1, starting transfers between devices: none -> 6.96 us  [total_of(): lax.all_to_all(jnp.stack([own] * lax.axis_size(axis)), axis, 0, 0)]
  transfers between devices with their start and end apart: 16 -> 13, of which waited for: 15 -> 12; matrix products, arithmetic and copies ran while one was open for 7% -> 8% of each run, Pallas kernels for 0% -> 0%
where the time goes in v1:
time: 603 us; the launch traced here: 595 us
  waiting for transfers between devices  252 us (42%)
  blocking collectives  186 us (31%)
  matrix products  55.1 us (9%)
  between operations  27.6 us (5%)
  local copies, waits for them, and re-layouts  26.4 us (4%)
  other arithmetic  24.4 us (4%)
  starting transfers between devices  23 us (4%)
    all_gather x5, waiting for transfers between devices, gathered_by_axis(): nearer = lax.all_gather(array, axes[-1], axis=dim, tiled=True)  147 us
    all_to_all x4, blocking collectives, total_of(): lax.all_to_all(jnp.stack([own] * lax.axis_size(axis)), axis, 0, 0)  120 us
    reduce_scatter x5, waiting for transfers between devices, total_of(): own = lax.psum_scatter(padded, axis, scatter_dimension=0, tiled=True)  85.1 us
    all_gather x5, blocking collectives, gathered_by_axis(): nearer = lax.all_gather(array, axes[-1], axis=dim, tiled=True)  65.7 us
    dot_general x5, matrix products, contract(): return jnp.einsum('tiw,tin->wn', panel_piece, selected, precision=HIGHEST)  34 us
    dot_general x6, matrix products, body(): jnp.dot(lower_inv[current_sup].T, right, precision=HIGHEST, preferred_ele...  21.1 us
    all_to_all x2, starting transfers between devices, from_everyone(): return lax.all_to_all(copies, axis, split_axis=0, concat_axis=0, tiled=True)  15.5 us
  transfers between devices with their start and end apart: 13, of which 12 were waited for; matrix products, arithmetic and copies ran while one was open for 8% of the time, Pallas kernels for 0%

profile of v1, /device:TPU:8, one launch (start us, length us, event | category | flops | bytes accessed | tf_op | source)
XLA Modules:
  0.0 595.0 jit_solution(18023636908558563428)
XLA Ops:
  20.2 13.1 %all_gather.30 = f32[2,256,256]{1,0,2:T(2,128)S(1)} all-gather(f32[2,256,64]{1,0,2:T(2,128)S(1)} %pad_maximum_fusion), channel_id=1, replica_groups=mesh['row'=8,'col_0'=8,'col_1'=4] {'col_1'}, dimensions={2}, use_global_device_ids=true | all-gather | bytes 655360 | tf_op jit(solution)/shard_map/all_gather | solution.py:45
  41.2 10.7 %broadcast_select_fusion = f32[6,2048,256]{2,1,0:T(8,128)} fusion(f32[6,2048,256]{2,1,0:T(8,128)} %param.18, pred[2048,256]{1,0:T(8,128)(4,1)S(1)} %iota_compare_fusion), kind=kLoop, calls=%fused_computation | loop fusion | flops 3145728 | bytes 25690112 | tf_op jit(solution)/shard_map/jit(_where)/select_n | solution.py:83
  55.7 36.5 %all-gather.6.cloned.1.call-done = f32[2,256,2048]{2,1,0:T(8,128)} async-done(((f32[2,256,256]{2,1,0:T(8,128)}), f32[2,256,2048]{2,1,0:T(8,128)}) %all-gather.6.cloned.1.call-update) | async-done | bytes 4194320 | tf_op jit(solution)/shard_map/all_gather | solution.py:45
  104.3 13.1 %all_gather.32 = f32[2,256,256]{1,0,2:T(2,128)S(1)} all-gather(f32[2,256,64]{1,0,2:T(2,128)S(1)} %pad_maximum_fusion.1), channel_id=1, replica_groups=mesh['row'=8,'col_0'=8,'col_1'=4] {'col_1'}, dimensions={2}, use_global_device_ids=true | all-gather | bytes 655360 | tf_op jit(solution)/shard_map/all_gather | solution.py:45
  118.4 9.6 %reduce-scatter.6.cloned.1.call-done = f32[256,66]{0,1:T(8,128)} async-done(((f32[2048,66]{0,1:T(8,128)}), f32[256,66]{0,1:T(8,128)}) %reduce-scatter.6.cloned.1.call-update) | async-done | bytes 67600 | tf_op jit(solution)/shard_map/reduce_scatter | solution.py:35
  137.9 8.4 %all-to-all-done.1 = f32[8,256,66]{1,2,0:T(8,128)S(1)} async-done(((f32[8,256,66]{1,2,0:T(8,128)}), f32[8,256,66]{1,2,0:T(8,128)S(1)}, u32[]{:S(2)}, u32[]{:S(2)}) %all-to-all-start.1) | async-done | bytes 540704 | tf_op jit(solution)/shard_map/all_to_all | solution.py:37
  150.1 36.1 %all-gather.8.cloned.1.call-done = f32[2,256,2048]{2,1,0:T(8,128)} async-done(((f32[2,256,256]{2,1,0:T(8,128)}), f32[2,256,2048]{2,1,0:T(8,128)}) %all-gather.8.cloned.1.call-update) | async-done | bytes 4194320 | tf_op jit(solution)/shard_map/all_gather | solution.py:45
  192.1 13.1 %all_gather.34 = f32[2,256,256]{1,0,2:T(2,128)S(1)} all-gather(f32[2,256,64]{1,0,2:T(2,128)S(1)} %pad_maximum_fusion.2), channel_id=1, replica_groups=mesh['row'=8,'col_0'=8,'col_1'=4] {'col_1'}, dimensions={2}, use_global_device_ids=true | all-gather | bytes 655360 | tf_op jit(solution)/shard_map/all_gather | solution.py:45
  206.3 16.3 %reduce-scatter.8.cloned.1.call-done = f32[256,130]{0,1:T(8,128)} async-done(((f32[2048,130]{0,1:T(8,128)}), f32[256,130]{0,1:T(8,128)}) %reduce-scatter.8.cloned.1.call-update) | async-done | bytes 133136 | tf_op jit(solution)/shard_map/reduce_scatter | solution.py:35
  223.5 21.3 %all_to_all.35 = f32[8,256,130]{1,2,0:T(8,128)S(1)} all-to-all(f32[8,256,130]{1,2,0:T(8,128)S(1)} %stack.59), channel_id=1, replica_groups=mesh['row'=8,'col_0'=8,'col_1'=4] {'row'}, dimensions={0} | all-to-all | bytes 2129920 | tf_op jit(solution)/shard_map/all_to_all | solution.py:37
  249.1 31.7 %all-gather.10.cloned.1.call-done = f32[2,256,2048]{2,1,0:T(8,128)} async-done(((f32[2,256,256]{2,1,0:T(8,128)}), f32[2,256,2048]{2,1,0:T(8,128)}) %all-gather.10.cloned.1.call-update) | async-done | bytes 4194320 | tf_op jit(solution)/shard_map/all_gather | solution.py:45
  295.2 13.3 %all_gather.36 = f32[2,256,256]{1,0,2:T(2,128)S(1)} all-gather(f32[2,256,64]{1,0,2:T(2,128)S(1)} %pad_maximum_fusion.3), channel_id=1, replica_groups=mesh['row'=8,'col_0'=8,'col_1'=4] {'col_1'}, dimensions={2}, use_global_device_ids=true | all-gather | bytes 655360 | tf_op jit(solution)/shard_map/all_gather | solution.py:45
  309.6 9.2 %reduce-scatter.10.cloned.1.call-done = f32[256,194]{0,1:T(8,128)} async-done(((f32[2048,194]{0,1:T(8,128)}), f32[256,194]{0,1:T(8,128)}) %reduce-scatter.10.cloned.1.call-update) | async-done | bytes 198672 | tf_op jit(solution)/shard_map/reduce_scatter | solution.py:35
  319.8 27.1 %all_to_all.36 = f32[8,256,194]{1,2,0:T(8,128)S(1)} all-to-all(f32[8,256,194]{1,2,0:T(8,128)S(1)} %stack.64), channel_id=1, replica_groups=mesh['row'=8,'col_0'=8,'col_1'=4] {'row'}, dimensions={0} | all-to-all | bytes 3178496 | tf_op jit(solution)/shard_map/all_to_all | solution.py:37
  352.1 25.2 %all-gather.12.cloned.1.call-done = f32[2,256,2048]{2,1,0:T(8,128)} async-done(((f32[2,256,256]{2,1,0:T(8,128)}), f32[2,256,2048]{2,1,0:T(8,128)}) %all-gather.12.cloned.1.call-update) | async-done | bytes 4194320 | tf_op jit(solution)/shard_map/all_gather | solution.py:45
  385.8 13.1 %all_gather.38 = f32[2,256,256]{1,0,2:T(2,128)S(1)} all-gather(f32[2,256,64]{1,0,2:T(2,128)S(1)} %pad_maximum_fusion.4), channel_id=1, replica_groups=mesh['row'=8,'col_0'=8,'col_1'=4] {'col_1'}, dimensions={2}, use_global_device_ids=true | all-gather | bytes 655360 | tf_op jit(solution)/shard_map/all_gather | solution.py:45
  400.0 17.0 %reduce-scatter.12.cloned.1.call-done = f32[256,258]{0,1:T(8,128)} async-done(((f32[2048,258]{0,1:T(8,128)}), f32[256,258]{0,1:T(8,128)}) %reduce-scatter.12.cloned.1.call-update) | async-done | bytes 264208 | tf_op jit(solution)/shard_map/reduce_scatter | solution.py:35
  418.1 33.3 %all_to_all.37 = f32[8,256,258]{1,2,0:T(8,128)S(1)} all-to-all(f32[8,256,258]{1,2,0:T(8,128)S(1)} %stack.69), channel_id=1, replica_groups=mesh['row'=8,'col_0'=8,'col_1'=4] {'row'}, dimensions={0} | all-to-all | bytes 4227072 | tf_op jit(solution)/shard_map/all_to_all | solution.py:37
  458.3 17.3 %all-gather.14.cloned.1.call-done = f32[2,256,2048]{2,1,0:T(8,128)} async-done(((f32[2,256,256]{2,1,0:T(8,128)}), f32[2,256,2048]{2,1,0:T(8,128)}) %all-gather.14.cloned.1.call-update) | async-done | bytes 4194320 | tf_op jit(solution)/shard_map/all_gather | solution.py:45
  475.6 8.4 %convolution_bitcast_fusion = f32[2048,322]{0,1:T(8,128)} fusion(f32[2,256,2048]{2,1,0:T(8,128)} %all-gather.14.cloned.1.call-done, f32[1,256,322]{1,2,0:T(8,128)S(1)} %slice_bitcast_fusion.34, f32[1,256,322]{1,2,0:T(8,128)} %slice_bitcast_fusion.35), kind=kOutput, calls=%fused_computation.8 | convolution fusion | flops 4051862528 | bytes 7491584 | tf_op jit(solution)/shard_map/tiw,tin->wn/dot_general | solution.py:55
  483.9 33.1 %reduce-scatter.14.cloned.1.call-done = f32[256,322]{0,1:T(8,128)} async-done(((f32[2048,322]{0,1:T(8,128)}), f32[256,322]{0,1:T(8,128)}) %reduce-scatter.14.cloned.1.call-update) | async-done | bytes 329744 | tf_op jit(solution)/shard_map/reduce_scatter | solution.py:35
  518.2 38.8 %all_to_all.38 = f32[8,256,322]{1,2,0:T(8,128)S(1)} all-to-all(f32[8,256,322]{1,2,0:T(8,128)S(1)} %stack.74), channel_id=1, replica_groups=mesh['row'=8,'col_0'=8,'col_1'=4] {'row'}, dimensions={0} | all-to-all | bytes 5275648 | tf_op jit(solution)/shard_map/all_to_all | solution.py:37
  564.9 9.8 %all-to-all-start.6 = ((f32[32,6,256]{2,1,0:T(8,128)}), f32[32,6,256]{2,1,0:T(8,128)S(1)}, u32[]{:S(2)}, u32[]{:S(2)}) async-start(f32[32,6,256]{2,1,0:T(8,128)} %broadcast_in_dim.18), calls=%async_computation.11 | async-start | bytes 524288 | tf_op jit(solution)/shard_map/all_to_all | solution.py:20
  575.3 12.0 %all-to-all-done.6 = f32[32,6,256]{2,1,0:T(8,128)S(1)} async-done(((f32[32,6,256]{2,1,0:T(8,128)}), f32[32,6,256]{2,1,0:T(8,128)S(1)}, u32[]{:S(2)}, u32[]{:S(2)}) %all-to-all-start.6) | async-done | bytes 196640 | tf_op jit(solution)/shard_map/all_to_all | solution.py:20
  (130 shorter events, 100.2 us)
Async XLA Ops:
  7.2 85.0 %all-gather.6.cloned.1.call-start = ((), (), s32[]{:S(2)}) async-start(), calls=%async_computation.12 | async-start | bytes 4718592 | tf_op jit(solution)/shard_map/all_gather | solution.py:45
  20.0 14.4 %copy-start.6 = (f32[6,256,2]{1,2,0:T(2,128)S(1)}, f32[6,256,2]{1,2,0:T(2,128)}, u32[]{:S(2)}) copy-start(f32[6,256,2]{1,2,0:T(2,128)} %param.21) | copy-start | bytes 36868
  35.1 16.9 %all-to-all-start = ((f32[8,6,256,2]{2,3,1,0:T(2,128)}), f32[8,6,256,2]{2,3,1,0:T(2,128)S(1)}, u32[]{:S(2)}, u32[]{:S(2)}) async-start(f32[8,6,256,2]{2,3,1,0:T(2,128)} %broadcast_in_dim.16), calls=%async_computation | async-start | bytes 196608 | tf_op jit(solution)/shard_map/all_to_all | solution.py:20
  40.8 87.2 %reduce-scatter.6.cloned.1.call-start = ((), (), s32[]{:S(2)}) async-start(), calls=%async_computation.13 | async-start | bytes 663552 | tf_op jit(solution)/shard_map/reduce_scatter | solution.py:35
  55.5 42.4 %copy-start = (f32[1,256,66]{1,2,0:T(8,128)}, f32[1,256,66]{1,2,0:T(8,128)S(1)}, u32[]{:S(2)}) copy-start(f32[1,256,66]{1,2,0:T(8,128)S(1)} %fusion.53) | copy-start | bytes 202756
  98.0 88.2 %all-gather.8.cloned.1.call-start = ((), (), s32[]{:S(2)}) async-start(), calls=%async_computation.14 | async-start | bytes 4718592 | tf_op jit(solution)/shard_map/all_gather | solution.py:45
  129.7 16.5 %all-to-all-start.1 = ((f32[8,256,66]{1,2,0:T(8,128)}), f32[8,256,66]{1,2,0:T(8,128)S(1)}, u32[]{:S(2)}, u32[]{:S(2)}) async-start(f32[8,256,66]{1,2,0:T(8,128)} %stack.54), calls=%async_computation.2 | async-start | bytes 1179648 | tf_op jit(solution)/shard_map/all_to_all | solution.py:37
  136.7 85.9 %reduce-scatter.8.cloned.1.call-start = ((), (), s32[]{:S(2)}) async-start(), calls=%async_computation.15 | async-start | bytes 1253376 | tf_op jit(solution)/shard_map/reduce_scatter | solution.py:35
  146.3 0.7 copy-start.5
  150.1 41.9 %copy-start.1 = (f32[1,256,64]{1,0,2:T(1,128)S(1)}, f32[1,256,64]{1,0,2:T(1,128)}, u32[]{:S(2)}) copy-start(f32[1,256,64]{1,0,2:T(1,128)} %get-tuple-element.91) | copy-start | bytes 196612
  150.1 41.9 %copy-start.2 = (f32[1,256,64]{1,0,2:T(1,128)S(1)}, f32[1,256,64]{1,0,2:T(1,128)}, u32[]{:S(2)}) copy-start(f32[1,256,64]{1,0,2:T(1,128)} %get-tuple-element.92) | copy-start | bytes 196612
  191.9 88.9 %all-gather.10.cloned.1.call-start = ((), (), s32[]{:S(2)}) async-start(), calls=%async_computation.16 | async-start | bytes 4718592 | tf_op jit(solution)/shard_map/all_gather | solution.py:45
  206.3 112.5 %reduce-scatter.10.cloned.1.call-start = ((), (), s32[]{:S(2)}) async-start(), calls=%async_computation.17 | async-start | bytes 1843200 | tf_op jit(solution)/shard_map/reduce_scatter | solution.py:35
  287.5 89.8 %all-gather.12.cloned.1.call-start = ((), (), s32[]{:S(2)}) async-start(), calls=%async_computation.18 | async-start | bytes 4718592 | tf_op jit(solution)/shard_map/all_gather | solution.py:45
  309.5 107.5 %reduce-scatter.12.cloned.1.call-start = ((), (), s32[]{:S(2)}) async-start(), calls=%async_computation.19 | async-start | bytes 2433024 | tf_op jit(solution)/shard_map/reduce_scatter | solution.py:35
  347.5 0.7 copy-start.4
  384.8 90.7 %all-gather.14.cloned.1.call-start = ((), (), s32[]{:S(2)}) async-start(), calls=%async_computation.20 | async-start | bytes 4718592 | tf_op jit(solution)/shard_map/all_gather | solution.py:45
  400.0 117.1 %reduce-scatter.14.cloned.1.call-start = ((), (), s32[]{:S(2)}) async-start(), calls=%async_computation.21 | async-start | bytes 3022848 | tf_op jit(solution)/shard_map/reduce_scatter | solution.py:35
  452.2 0.9 copy-start.3
  564.9 22.4 %all-to-all-start.6 = ((f32[32,6,256]{2,1,0:T(8,128)}), f32[32,6,256]{2,1,0:T(8,128)S(1)}, u32[]{:S(2)}, u32[]{:S(2)}) async-start(f32[32,6,256]{2,1,0:T(8,128)} %broadcast_in_dim.18), calls=%async_computation.11 | async-start | bytes 524288 | tf_op jit(solution)/shard_map/all_to_all | solution.py:20
Sparse Core Ops, SparseCore 0:
  34.5 57.5 all-gather.5
  98.1 29.8 reduce-scatter.5
  129.8 56.3 all-gather.7
  192.0 30.4 reduce-scatter.7
  224.2 56.5 all-gather.9
  287.6 31.1 reduce-scatter.9
  320.5 56.7 all-gather.11
  384.9 32.0 reduce-scatter.11
  418.8 56.7 all-gather.13
  484.1 32.9 reduce-scatter.13
